TPU v7x, 32 devices: a whole 2x2x4 slice. The times are simulated.
32 devices in a mesh: section: 4 (over y, x), vocab: 2 (over core), dp: 4 (over z).
Axes of the slice: x: 2, y: 2, z: 4, core: 2. Of those that a mesh axis runs over, the one named last changes fastest.
Arguments:
- entering: bfloat16 [8, 4, 32, 2048], P(None, 'dp', 'vocab'), may hold values from -6 to 6
- depths: int32 [8], replicated, may hold values from 1 to 4
- targets: int32 [8, 4, 32], P(None, 'dp'), may hold values from 0 to 64127
- norm_gain: float32 [4, 2048], P('section'), may hold values from 0.5 to 1.5
- w_gate: bfloat16 [4, 2048, 7168], P('section', 'dp', 'vocab'), may hold values from -0.125 to 0.125
- w_up: bfloat16 [4, 2048, 7168], P('section', 'dp', 'vocab'), may hold values from -0.125 to 0.125
- w_down: bfloat16 [4, 7168, 2048], P('section', 'vocab', 'dp'), may hold values from -0.0625 to 0.0625
- final_gain: float32 [2048], replicated, may hold values from 0.5 to 1.5
- head_weight: bfloat16 [2048, 64128], P(None, ('section', 'vocab')), may hold values from -32 to 32
Outputs:
- token_loss: float32 [8, 4, 32], P(None, 'dp')
- mean_loss: float32 [], replicated
All inputs are finite; a program needn't handle non-finite values.
Results may differ from a plain program's by a relative error of at most 0.0055.
Values may be sent and summed in bfloat16 or wider, within the bound.
No kernel may reach another device: no remote copies, remote signals or barrier semaphores. Data moves between devices by JAX's collectives and lax.ppermute only.
A program may use at most 192 MiB of HBM per device.

v0:
```python
import jax
import jax.numpy as jnp
from jax import lax
from jax.experimental import pallas as pl
from jax.experimental.pallas import tpu as pltpu
from jax.sharding import PartitionSpec as P


EPS = 1e-05
MESH_AXES = ("section", "vocab", "dp")


def rms_scaled(values, gain):
    widened = values.astype(jnp.float32)
    return widened * lax.rsqrt(jnp.mean(widened * widened, axis=-1, keepdims=True) + EPS) * gain


def combine_rows(first_stats, second_stats):
    peak_one, total_one, picked_one = first_stats
    peak_two, total_two, picked_two = second_stats
    peak_new = jnp.maximum(peak_one, peak_two)
    total_new = total_one * jnp.exp(peak_one - peak_new) + total_two * jnp.exp(peak_two - peak_new)
    return (peak_new, total_new, picked_one + picked_two)


def swapped(block, axis, mask, targets=None):
    size = lax.axis_size(axis)
    pairs = [(i, i ^ mask) for i in range(size) if targets is None or (i ^ mask) in targets]
    return lax.ppermute(block, axis, pairs)


def chosen(options, index):
    result = options[0]
    for k in range(1, len(options)):
        result = jnp.where(index == k, options[k], result)
    return result


def absolute(values, index, axis, size):
    bit = 1
    while bit < size:
        flipped = jnp.concatenate(
            [lax.index_in_dim(values, i ^ bit, axis, True) for i in range(size)], axis
        )
        values = jnp.where((index & bit) != 0, flipped, values)
        bit *= 2
    return values


def after(value, *others):
    return lax.optimization_barrier((value,) + others)[0]


def layer_body(plane, *refs, pieces, blocks, steps):
    rows, refs = refs[:pieces], refs[pieces:]
    gates, ups, downs = refs[:blocks], refs[blocks : 2 * blocks], refs[2 * blocks : 3 * blocks]
    refs = refs[3 * blocks :]
    kept, sent = refs[: pieces // 2], refs[pieces // 2 : pieces]
    gathered, total = refs[pieces:]
    each = rows[0].shape[0]
    features = gates[0].shape[0]
    step = pl.program_id(0)

    def place(mask):
        return pl.ds(pl.multiple_of((plane[0] ^ mask) * features, features), features)

    @pl.when(step == 0)
    def _():
        for i in range(pieces):
            for mask in range(blocks):
                gathered[pl.ds(i * each, each), mask * features : (mask + 1) * features] = rows[i][
                    :, place(mask)
                ]

    count = pieces * each
    tile = min(count, 256)

    def tile_products(index, carry):
        first = pl.multiple_of(index * tile, tile)

        def product(matrices):
            result = None
            for mask in range(blocks):
                here = gathered[pl.ds(first, tile), mask * features : (mask + 1) * features]
                part = jnp.dot(here, matrices[mask][...], preferred_element_type=jnp.float32)
                result = part if result is None else result + part
            return result

        gate_part = product(gates)
        up_part = product(ups)
        hidden = (gate_part / (1.0 + jnp.exp(-gate_part)) * up_part).astype(jnp.bfloat16)
        for mask in range(blocks):
            part = jnp.dot(hidden, downs[mask][...], preferred_element_type=jnp.float32)
            columns = slice(mask * features, (mask + 1) * features)

            @pl.when(step == 0)
            def _(part=part, columns=columns):
                total[pl.ds(first, tile), columns] = part

            @pl.when(step > 0)
            def _(part=part, columns=columns):
                total[pl.ds(first, tile), columns] += part

        return carry

    lax.fori_loop(0, count // tile, tile_products, 0)

    @pl.when(step == steps - 1)
    def _():
        for i in range(pieces):
            for mask in range(blocks):
                block = total[pl.ds(i * each, each), mask * features : (mask + 1) * features]
                if i < pieces // 2:
                    kept[i][:, place(mask)] = block
                else:
                    sent[i - pieces // 2][:, place(mask)] = block.astype(jnp.bfloat16)


def layer_products(rows, weights, plane):
    gates, ups, downs = weights
    pieces, blocks = len(rows), len(gates)
    each, width = rows[0].shape
    features, hidden = gates[0].shape
    steps = 2 if hidden % 256 == 0 else 1
    part = hidden // steps
    whole = pl.BlockSpec((each, width), lambda i, plane: (0, 0))
    results = pl.pallas_call(
        lambda *refs: layer_body(*refs, pieces=pieces, blocks=blocks, steps=steps),
        grid_spec=pltpu.PrefetchScalarGridSpec(
            num_scalar_prefetch=1,
            grid=(steps,),
            in_specs=[whole] * pieces
            + [pl.BlockSpec((features, part), lambda i, plane: (0, i))] * (2 * blocks)
            + [pl.BlockSpec((part, features), lambda i, plane: (i, 0))] * blocks,
            out_specs=[whole] * pieces,
            scratch_shapes=[
                pltpu.VMEM((pieces * each, width), jnp.bfloat16),
                pltpu.VMEM((pieces * each, width), jnp.float32),
            ],
        ),
        out_shape=[jax.ShapeDtypeStruct((each, width), jnp.float32)] * (pieces // 2)
        + [jax.ShapeDtypeStruct((each, width), jnp.bfloat16)] * (pieces - pieces // 2),
        compiler_params=pltpu.CompilerParams(
            dimension_semantics=("arbitrary",), vmem_limit_bytes=60 * 1024 * 1024
        ),
        cost_estimate=pl.CostEstimate(
            flops=6 * pieces * each * width * hidden,
            bytes_accessed=6 * width * hidden + 5 * pieces * each * width,
            transcendentals=pieces * each * hidden,
        ),
        name="layer_products",
    )(plane, *rows, *gates, *ups, *downs)
    return results[: pieces // 2], results[pieces // 2 :]


def head_body(*refs, pieces, columns, tile, lines):
    rows = refs[:pieces]
    labels, weight = refs[pieces : pieces + 2]
    stats_out = refs[pieces + 2]
    gathered, turned, peak, total, picked = refs[pieces + 3 :]
    each = rows[0].shape[0]
    step = pl.program_id(0)
    steps = pl.num_programs(0)

    @pl.when(step == 0)
    def _():
        for i in range(pieces):
            gathered[pl.ds(i * each, each), :] = rows[i][...]
        turned[...] = gathered[...].T
        peak[...] = jnp.full(peak.shape, -1e30, jnp.float32)
        total[...] = jnp.zeros(total.shape, jnp.float32)
        picked[...] = jnp.zeros(picked.shape, jnp.float32)

    count = pieces * each
    some = min(count, 256)
    for first in range(0, count, some):
        span = slice(first, first + some)
        logits = jnp.dot(weight[...], turned[:, span], preferred_element_type=jnp.float32)
        place = step * tile + lax.broadcasted_iota(jnp.int32, (tile, some), 0)
        found = jnp.where(place == labels[:, span], logits, 0.0)
        logits = jnp.where(place < columns, logits, -1e30)
        groups = [slice(i * lines, (i + 1) * lines) for i in range(tile // lines)]
        highest = peak[:, span]
        gained = picked[:, span]
        for group in groups:
            highest = jnp.maximum(highest, logits[group])
            gained = gained + found[group]
        sums = total[:, span] * jnp.exp(peak[:, span] - highest)
        for group in groups:
            sums = sums + jnp.exp(logits[group] - highest)
        peak[:, span] = highest
        total[:, span] = sums
        picked[:, span] = gained

    @pl.when(step == steps - 1)
    def _():
        top = jnp.max(peak[...], axis=0, keepdims=True)
        stats_out[0:1, :] = top
        stats_out[1:2, :] = jnp.sum(total[...] * jnp.exp(peak[...] - top), axis=0, keepdims=True)
        stats_out[2:3, :] = jnp.sum(picked[...], axis=0, keepdims=True)


def head_stats(rows, labels, weight):
    pieces = len(rows)
    each, width = rows[0].shape
    columns = weight.shape[0]
    tile, lines = 512, 8
    count = pieces * each
    whole = pl.BlockSpec((each, width), lambda i: (0, 0))
    return pl.pallas_call(
        lambda *refs: head_body(*refs, pieces=pieces, columns=columns, tile=tile, lines=lines),
        grid=(pl.cdiv(columns, tile),),
        in_specs=[whole] * pieces
        + [
            pl.BlockSpec((1, count), lambda i: (0, 0)),
            pl.BlockSpec((tile, width), lambda i: (i, 0)),
        ],
        out_specs=pl.BlockSpec((3, count), lambda i: (0, 0)),
        out_shape=jax.ShapeDtypeStruct((3, count), jnp.float32),
        scratch_shapes=[
            pltpu.VMEM((count, width), jnp.bfloat16),
            pltpu.VMEM((width, count), jnp.bfloat16),
        ]
        + [pltpu.VMEM((lines, count), jnp.float32)] * 3,
        compiler_params=pltpu.CompilerParams(
            dimension_semantics=("arbitrary",), vmem_limit_bytes=60 * 1024 * 1024
        ),
        cost_estimate=pl.CostEstimate(
            flops=2 * count * width * columns,
            bytes_accessed=2 * width * columns + 2 * count * width,
            transcendentals=count * columns,
        ),
        name="head_stats",
    )(*rows, labels, weight)


def by_planes(*args):
    return planes_step(*args)


def planes_step(entering, depths, targets, norm_gain, w_gate, w_up, w_down, final_gain, head_weight):
    sections = lax.axis_size("section")
    cores = lax.axis_size("vocab")
    my_column = lax.axis_index("section")
    my_core = lax.axis_index("vocab")
    my_plane = lax.axis_index("dp")
    micro_count, _, rows_each, width = entering.shape
    layers = sections
    first_plane = sections // 2 - 1
    plane_of = [(first_plane + layer) % sections for layer in range(layers)]
    my_layer = (my_plane - first_plane) % sections

    def linear(section, core, plane):
        return (section * cores + core) * sections + plane

    micro_ids = jnp.arange(micro_count, dtype=jnp.int32)
    deeper = (depths[None, :] > depths[:, None]) | (
        (depths[None, :] == depths[:, None]) & (micro_ids[None, :] < micro_ids[:, None])
    )
    rank = jnp.sum(deeper.astype(jnp.int32), axis=1)
    hot = rank[None, :] == micro_ids[:, None]
    order = jnp.sum(jnp.where(hot, micro_ids[None, :], 0), axis=1)
    sorted_depths = jnp.sum(jnp.where(hot, depths[None, :], 0), axis=1)
    active_counts = [jnp.sum((depths > layer).astype(jnp.int32)) for layer in range(layers + 1)]

    hidden_each = w_gate.shape[2] // sections

    def column_block(matrix, column):
        if matrix is w_down:
            return lax.dynamic_slice_in_dim(matrix[0], column * hidden_each, hidden_each, 0)
        return lax.dynamic_slice_in_dim(matrix[0], column * hidden_each, hidden_each, 1)

    def across(matrix):
        return [
            swapped(column_block(matrix, my_column ^ mask), "section", mask)
            if mask
            else column_block(matrix, my_column)
            for mask in range(sections)
        ]

    def layer_at(plane):
        return (plane - first_plane) % sections

    early_planes = plane_of[:2]
    late_planes = plane_of[2:]

    def blocks_for(held):
        return [chosen(held, layer_at(my_plane ^ mask) ^ my_column) for mask in range(sections)]

    def towards(blocks, planes, *earlier):
        return [
            swapped(after(blocks[mask], *earlier), "dp", mask, planes) if mask else blocks[0]
            for mask in range(sections)
        ]

    gates = across(w_gate)
    ups = across(w_up)
    downs = across(w_down)
    gates = blocks_for(gates)
    gates_early = towards(gates, early_planes)
    ups = blocks_for(ups)
    ups_early = towards(ups, early_planes)
    downs = blocks_for(downs)
    downs_early = towards(downs, early_planes)
    gates_late = towards(gates, late_planes, *downs_early[1:])
    early = (gates_early, ups_early, downs_early)

    gains = [norm_gain] + [swapped(norm_gain, "section", mask) for mask in range(1, sections)]
    my_gain = chosen(gains, my_layer ^ my_column)
    labels_by = [targets[:, 0]] + [
        swapped(targets[:, 0], "dp", mask) for mask in range(1, sections)
    ]
    labels_all = absolute(jnp.stack(labels_by), my_plane, 0, sections)

    def spread_rows(rows):
        own = [rows] + [swapped(rows, "section", mask) for mask in range(1, sections)]
        return own + [swapped(piece, "vocab", 1) for piece in own]

    def collected(kept, sent):
        total = None
        for mask in reversed(range(sections)):
            both = kept[mask] + swapped(sent[mask], "vocab", 1).astype(jnp.float32)
            if mask:
                both = swapped(both.astype(jnp.bfloat16), "section", mask).astype(jnp.float32)
            total = both if total is None else total + both
        return total

    def run_layer(layer, state, weights, count):
        current = state[:count].reshape(count * rows_each, width)
        rows = spread_rows(rms_scaled(current, my_gain).astype(jnp.bfloat16))
        branch = collected(*layer_products(rows, weights, my_plane[None]))
        moved = (current.astype(jnp.float32) + branch).astype(jnp.bfloat16)
        keep = (sorted_depths[:count] > layer)[:, None, None]
        moved = jnp.where(keep, moved.reshape(count, rows_each, width), state[:count])
        if count < micro_count:
            moved = jnp.concatenate([moved, state[count:]], 0)
        return moved

    def handed_on(state, layer, count):
        pairs = [
            (linear(s, c, plane_of[layer - 1]), linear(s, c, plane_of[layer]))
            for s in range(sections)
            for c in range(cores)
        ]
        arrived = lax.ppermute(state[:count], MESH_AXES, pairs)
        if count < micro_count:
            arrived = jnp.concatenate([arrived, state[count:]], 0)
        return jnp.where(my_plane == plane_of[layer], arrived, state)

    sorted_rows = jnp.concatenate(
        [lax.dynamic_slice_in_dim(entering[:, 0], order[i], 1, 0) for i in range(micro_count)], 0
    )
    pairs = [
        (linear(s, c, s), linear(s, c, plane_of[0])) for s in range(sections) for c in range(cores)
    ]
    state = lax.ppermute(after(sorted_rows, labels_all), MESH_AXES, pairs)
    state = run_layer(0, state, early, micro_count)
    state = handed_on(state, 1, micro_count)
    word = state[0, :8, :128].astype(jnp.float32)
    pairs = [
        (linear(s, c, source), linear(s, c, source ^ 1))
        for s in range(sections)
        for c in range(cores)
        for source in early_planes
    ]
    word = lax.ppermute(word, MESH_AXES, pairs)
    ups_late = towards(ups, late_planes, state, word)
    downs_late = towards(downs, late_planes, state, word)
    late_blocks = (gates_late, ups_late, downs_late)
    sizes = [n for n in range(2, micro_count + 1, 2)]
    for layer in range(1, layers):
        if layer == 2:
            state, late_blocks = lax.optimization_barrier((state, late_blocks))
        weights = early if layer < 2 else late_blocks

        def branch_of(count, layer=layer):
            def run(state, weights):
                if layer > 1:
                    state = handed_on(state, layer, count)
                return run_layer(layer, state, weights, count)

            return run

        which = jnp.clip((active_counts[layer] + 1) // 2 - 1, 0, len(sizes) - 1)
        state = lax.switch(which, [branch_of(n) for n in sizes], state, weights)

    exits_from = chosen(active_counts[1:], my_layer)
    exits_to = chosen(active_counts[:layers], my_layer)
    exit_count = exits_to - exits_from
    most = active_counts[0] - active_counts[1]
    for layer in range(1, layers):
        most = jnp.maximum(most, active_counts[layer] - active_counts[layer + 1])
    column_count = head_weight.shape[1]
    first_column = (my_column * cores + my_core) * column_count
    labels_sorted = jnp.concatenate(
        [lax.dynamic_slice_in_dim(labels_all, order[i], 1, 1) for i in range(micro_count)], 1
    )

    def head(count):
        def run(state, head_columns):
            def window(array, axis):
                padding = [(0, 0)] * array.ndim
                padding[axis] = (0, micro_count)
                return lax.dynamic_slice_in_dim(jnp.pad(array, padding), exits_from, count, axis)

            leaving = window(state, 0).reshape(count * rows_each, width)
            finals = rms_scaled(leaving, final_gain).astype(jnp.bfloat16)
            rows = spread_rows(finals)
            labels = window(labels_sorted, 1).reshape(sections, count, cores, rows_each)
            labels = labels.transpose(2, 0, 1, 3)
            labels = absolute(absolute(labels, my_core, 0, cores), my_column, 1, sections)
            labels = labels.reshape(1, -1) - first_column
            labels = jnp.where(labels < column_count, labels, -1)
            stats = head_stats(rows, labels, head_columns).reshape(3, cores, sections, -1)
            stats = absolute(absolute(stats, my_core, 1, cores), my_column, 2, sections)
            every = lax.all_gather(stats, ("section", "vocab"))
            joined = (every[0, 0], every[0, 1], every[0, 2])
            for i in range(1, sections * cores):
                joined = combine_rows(joined, (every[i, 0], every[i, 1], every[i, 2]))
            losses = jnp.log(joined[1]) + joined[0] - joined[2]
            losses = losses.reshape(cores, sections, count, rows_each).transpose(2, 1, 0, 3)
            losses = losses.reshape(count, sections, cores * rows_each)
            inside = jnp.arange(count) < exit_count
            losses = jnp.where(inside[:, None, None], losses, 0.0)
            table = jnp.zeros((2 * micro_count,) + losses.shape[1:], jnp.float32)
            table = lax.dynamic_update_slice_in_dim(table, losses, exits_from, 0)[:micro_count]
            return table

        return run

    which = jnp.clip((most + 1) // 2 - 1, 0, len(sizes) - 1)
    table = lax.switch(which, [head(n) for n in sizes], state, head_weight.T)
    for mask in (1, 2):
        table = table + swapped(table, "dp", mask)
    mean_loss = jnp.sum(table) / float(table.size)
    token_loss = jnp.sum(jnp.where(hot[:, :, None, None], table[:, None], 0.0), axis=0)
    token_loss = lax.dynamic_slice_in_dim(token_loss, my_plane, 1, 1)
    return (token_loss, mean_loss)


def passed_along(block, axis, distance):
    devices = range(lax.axis_size(axis))
    route = [(i - distance, i) for i in devices if i - distance in devices]
    return lax.ppermute(block, axis, route)


def spread(value, axis, source):
    kept = jnp.where(lax.axis_index(axis) == source, value, 0).astype(value.dtype)
    return lax.psum(kept, axis)


def joined(part, axis, combine):
    gathered = jax.tree.map(lambda a: lax.all_gather(a, axis), part)

    def take(source):
        return jax.tree.map(lambda a: lax.dynamic_index_in_dim(a, source, 0, False), gathered)

    return lax.fori_loop(
        1, lax.axis_size(axis), lambda source, state: combine(state, take(source)), take(0)
    )


def by_sections(entering, depths, targets, norm_gain, w_gate, w_up, w_down, final_gain, head_weight):
    segment_count = lax.axis_size("section")
    my_segment = lax.axis_index("section")
    micro_count = entering.shape[0]
    row_count = entering.shape[2]
    width = entering.shape[3]
    per_segment = w_gate.shape[0]
    gate_full, up_full, down_full = (
        lax.all_gather(w_gate, "dp", axis=1, tiled=True),
        lax.all_gather(w_up, "dp", axis=1, tiled=True),
        lax.all_gather(w_down, "dp", axis=2, tiled=True),
    )
    local_rows = entering[:, 0]

    def apply_layer(layer_index, current):
        normed = rms_scaled(current, norm_gain[layer_index]).astype(jnp.bfloat16)
        block_rows = lax.all_gather(normed, "vocab", axis=0, tiled=True)
        gate_part = jnp.dot(block_rows, gate_full[layer_index], preferred_element_type=jnp.float32)
        up_part = jnp.dot(block_rows, up_full[layer_index], preferred_element_type=jnp.float32)
        hidden = (jax.nn.silu(gate_part) * up_part).astype(jnp.bfloat16)
        branch = lax.psum_scatter(
            jnp.dot(hidden, down_full[layer_index], preferred_element_type=jnp.float32),
            "vocab",
            scatter_dimension=0,
            tiled=True,
        )
        return (current.astype(jnp.float32) + branch).astype(jnp.bfloat16)

    inject_order = jnp.arange(micro_count, dtype=jnp.int32)

    def advance(step_index, carry):
        current, kept_rows = carry
        slot_index = step_index - my_segment
        is_valid = (slot_index >= 0) & (slot_index < micro_count)
        member = inject_order[jnp.clip(slot_index, 0, micro_count - 1)]
        depth_now = jnp.where(is_valid, depths[member], 0)
        fresh_rows = lax.dynamic_index_in_dim(local_rows, member, 0, keepdims=False)
        current = jnp.where(my_segment == 0, fresh_rows, current)
        updated = apply_layer(0, current)
        current = jnp.where(my_segment * per_segment + 0 < depth_now, updated, current)
        record = is_valid & (my_segment == segment_count - 1)
        record_value = current
        previous = lax.dynamic_index_in_dim(kept_rows, member, 0, keepdims=False)
        kept_rows = lax.dynamic_update_index_in_dim(
            kept_rows, jnp.where(record, record_value, previous), member, 0
        )
        current = passed_along(current, "section", 1)
        return (current, kept_rows)

    start_rows = jnp.zeros((row_count, width), jnp.bfloat16)
    start_kept = jnp.zeros((micro_count, row_count, width), jnp.bfloat16)
    _, kept_rows = lax.fori_loop(
        0, micro_count + segment_count - 1, advance, (start_rows, start_kept)
    )
    finals = rms_scaled(kept_rows, final_gain).astype(jnp.bfloat16)
    finals = spread(finals, "section", segment_count - 1)
    share_rows = lax.all_gather(finals, "vocab", axis=1, tiled=True)
    labels = targets[:, 0]
    column_count = head_weight.shape[1]
    first_column = (my_segment * lax.axis_size("vocab") + lax.axis_index("vocab")) * column_count
    logits = jnp.einsum("mpd,dc->mpc", share_rows, head_weight, preferred_element_type=jnp.float32)
    columns = first_column + jnp.arange(column_count, dtype=jnp.int32)
    picked = jnp.sum(jnp.where(columns == labels[:, :, None], logits, 0.0), axis=-1)
    local_peak = jnp.max(logits, axis=-1)
    local_total = jnp.sum(jnp.exp(logits - local_peak[:, :, None]), axis=-1)
    peak_all, totals, target_logit = joined(
        (local_peak, local_total, picked), ("section", "vocab"), combine_rows
    )
    losses = jnp.log(totals) + peak_all - target_logit
    share_sum = lax.psum(jnp.sum(losses), "dp")
    mean_loss = share_sum / float(micro_count * lax.axis_size("dp") * losses.shape[1])
    return (losses[:, None, :], mean_loss)


def solution(mesh):
    in_specs = (
        P(None, "dp", "vocab", None),
        P(),
        P(None, "dp", None),
        P("section", None),
        P("section", "dp", "vocab"),
        P("section", "dp", "vocab"),
        P("section", "vocab", "dp"),
        P(),
        P(None, ("section", "vocab")),
    )
    out_specs = (P(None, "dp", None), P())
    square = mesh.shape["section"] == mesh.shape["dp"] == 4 and mesh.shape["vocab"] == 2
    return jax.shard_map(
        by_planes if square else by_sections,
        mesh=mesh,
        in_specs=in_specs,
        out_specs=out_specs,
        check_vma=False,
    )
```

profile of v0, /device:TPU:0, one launch (start us, length us, event | category | flops | bytes accessed | tf_op | source)
XLA Modules:
  0.0 790.1 jit_solution(14329264127742148872)
XLA Ops:
  70.5 18.7 %collective-permute-done.219 = bf16[512,896]{1,0:T(8,128)(2,1)} collective-permute-done((bf16[512,896]{1,0:T(8,128)(2,1)}, bf16[512,896]{1,0:T(8,128)(2,1)}, u32[]{:S(2)}, u32[]{:S(2)}) %collective-permute-start.219) | collective-permute-done | bytes 917536 | tf_op jit(solution)/shard_map/ppermute | solution.py:29
  92.3 15.2 %collective-permute-done.226 = bf16[512,896]{1,0:T(8,128)(2,1)} collective-permute-done((bf16[512,896]{1,0:T(8,128)(2,1)}, bf16[512,896]{1,0:T(8,128)(2,1)}, u32[]{:S(2)}, u32[]{:S(2)}) %collective-permute-start.226) | collective-permute-done | bytes 917536 | tf_op jit(solution)/shard_map/ppermute | solution.py:29
  109.9 18.7 %collective-permute-done.225 = bf16[512,896]{1,0:T(8,128)(2,1)} collective-permute-done((bf16[512,896]{1,0:T(8,128)(2,1)}, bf16[512,896]{1,0:T(8,128)(2,1)}, u32[]{:S(2)}, u32[]{:S(2)}) %collective-permute-start.225) | collective-permute-done | bytes 917536 | tf_op jit(solution)/shard_map/ppermute | solution.py:29
  130.1 16.7 %collective-permute-done.232 = bf16[896,512]{1,0:T(8,128)(2,1)} collective-permute-done((bf16[896,512]{1,0:T(8,128)(2,1)}, bf16[896,512]{1,0:T(8,128)(2,1)}, u32[]{:S(2)}, u32[]{:S(2)}) %collective-permute-start.232) | collective-permute-done | bytes 917536 | tf_op jit(solution)/shard_map/ppermute | solution.py:29
  146.8 32.3 %collective-permute-done.231 = bf16[896,512]{1,0:T(8,128)(2,1)} collective-permute-done((bf16[896,512]{1,0:T(8,128)(2,1)S(1)}, bf16[896,512]{1,0:T(8,128)(2,1)}, u32[]{:S(2)}, u32[]{:S(2)}) %collective-permute-start.231) | collective-permute-done | bytes 917536 | tf_op jit(solution)/shard_map/ppermute | solution.py:29
  216.6 18.0 %collective-permute-done.222.refs_11_ = bf16[512,896]{1,0:T(8,128)(2,1)} collective-permute-done((bf16[512,896]{1,0:T(8,128)(2,1)S(1)}, bf16[512,896]{1,0:T(8,128)(2,1)}, u32[]{:S(2)}, u32[]{:S(2)}) %collective-permute-start.222) | collective-permute-done | bytes 917536 | tf_op jit(solution)/shard_map/ppermute | solution.py:29
  243.7 10.6 %collective-permute-done.227.refs_14_ = bf16[512,896]{1,0:T(8,128)(2,1)} collective-permute-done((bf16[512,896]{1,0:T(8,128)(2,1)S(1)}, bf16[512,896]{1,0:T(8,128)(2,1)}, u32[]{:S(2)}, u32[]{:S(2)}) %collective-permute-start.227) | collective-permute-done | bytes 917536 | tf_op jit(solution)/shard_map/ppermute | solution.py:29
  256.0 18.0 %collective-permute-done.228.refs_15_ = bf16[512,896]{1,0:T(8,128)(2,1)} collective-permute-done((bf16[512,896]{1,0:T(8,128)(2,1)S(1)}, bf16[512,896]{1,0:T(8,128)(2,1)}, u32[]{:S(2)}, u32[]{:S(2)}) %collective-permute-start.228) | collective-permute-done | bytes 917536 | tf_op jit(solution)/shard_map/ppermute | solution.py:29
  274.0 19.7 %collective-permute-done.233.refs_18_ = bf16[896,512]{1,0:T(8,128)(2,1)} collective-permute-done((bf16[896,512]{1,0:T(8,128)(2,1)S(1)}, bf16[896,512]{1,0:T(8,128)(2,1)}, u32[]{:S(2)}, u32[]{:S(2)}) %collective-permute-start.233) | collective-permute-done | bytes 917536 | tf_op jit(solution)/shard_map/ppermute | solution.py:29
  293.7 19.2 %collective-permute-done.234.refs_19_ = bf16[896,512]{1,0:T(8,128)(2,1)} collective-permute-done((bf16[896,512]{1,0:T(8,128)(2,1)S(1)}, bf16[896,512]{1,0:T(8,128)(2,1)}, u32[]{:S(2)}, u32[]{:S(2)}) %collective-permute-start.234) | collective-permute-done | bytes 917536 | tf_op jit(solution)/shard_map/ppermute | solution.py:29
  312.9 21.8 %layer_products.25 = (f32[128,2048]{1,0:T(8,128)}, f32[128,2048]{1,0:T(8,128)}, f32[128,2048]{1,0:T(8,128)}, f32[128,2048]{1,0:T(8,128)}, bf16[128,2048]{1,0:T(8...) custom-call(s32[1]{0:T(128)} %bitcast.114.refs_0_, ...), custom_call_target="tpu_custom_call" | custom-call | flops 11274289152 | bytes 21495808 | tf_op jit(solution)/shard_map/layer_products/pallas_call | solution.py:127
  343.4 10.6 %collective-permute-done.237 = bf16[128,2048]{1,0:T(8,128)(2,1)S(1)} collective-permute-done((bf16[128,2048]{1,0:T(8,128)(2,1)S(1)}, bf16[128,2048]{1,0:T(8,128)(2,1)S(1)}, u32[]{:S(2)}, u32[]{:S(2)}) %collective-permute-start.237) | collective-permute-done | bytes 524320 | tf_op jit(solution)/shard_map/ppermute | solution.py:29
  354.1 10.4 %collective-permute-done.239 = bf16[128,2048]{1,0:T(8,128)(2,1)S(1)} collective-permute-done((bf16[128,2048]{1,0:T(8,128)(2,1)S(1)}, bf16[128,2048]{1,0:T(8,128)(2,1)S(1)}, u32[]{:S(2)}, u32[]{:S(2)}) %collective-permute-start.239) | collective-permute-done | bytes 524320 | tf_op jit(solution)/shard_map/ppermute | solution.py:29
  369.5 50.5 %conditional.4 = (bf16[8,16,2048]{2,1,0:T(8,128)(2,1)S(1)}) conditional(s32[]{:T(128)} %clamp.15, (s32[8]{0:T(128)S(1)}, bf16[8,16,2048]{2,1,0:T(8,128)(2,1)S(1)}, s32[]{:T(128)}, f32[1,2048]{1,0:T(1,128)S(1)}, bf16[512,896]{1,0:T(8,128)(2,1)S(1)}, /*index=5*/bf16[512,896]{1,0:T(8,128)(2,1)}, ...), branch_computations={%region_9.11_spmd, %region_11.13_spmd, %region_13.15_spmd, %region... | conditional | flops 11281629184 | bytes 89665408 | solution.py:385
  387.3 13.1 %layer_products.14 = (f32[64,2048]{1,0:T(8,128)}, f32[64,2048]{1,0:T(8,128)}, f32[64,2048]{1,0:T(8,128)}, f32[64,2048]{1,0:T(8,128)}, bf16[64,2048]{1,0:T(8,128)...) custom-call(s32[1]{0:T(128)} %bitcast.5.refs_0_, ...), custom_call_target="tpu_custom_call" | custom-call | flops 5637144576 | bytes 16252928 | tf_op jit(solution)/shard_map/cond/branch_1_fun/layer_products/pallas_call | solution.py:127
  434.2 78.4 %collective-permute-done.244 = bf16[512,896]{1,0:T(8,128)(2,1)} collective-permute-done((bf16[512,896]{1,0:T(8,128)(2,1)}, bf16[512,896]{1,0:T(8,128)(2,1)}, u32[]{:S(2)}, u32[]{:S(2)}) %collective-permute-start.244) | collective-permute-done | bytes 917536 | tf_op jit(solution)/shard_map/ppermute | solution.py:29
  519.6 52.1 %collective-permute-done.248 = bf16[512,896]{1,0:T(8,128)(2,1)} collective-permute-done((bf16[512,896]{1,0:T(8,128)(2,1)}, bf16[512,896]{1,0:T(8,128)(2,1)}, u32[]{:S(2)}, u32[]{:S(2)}) %collective-permute-start.248) | collective-permute-done | bytes 917536 | tf_op jit(solution)/shard_map/ppermute | solution.py:29
  582.7 28.2 %collective-permute-done.251 = bf16[896,512]{1,0:T(8,128)(2,1)} collective-permute-done((bf16[896,512]{1,0:T(8,128)(2,1)}, bf16[896,512]{1,0:T(8,128)(2,1)}, u32[]{:S(2)}, u32[]{:S(2)}) %collective-permute-start.251) | collective-permute-done | bytes 917536 | tf_op jit(solution)/shard_map/ppermute | solution.py:29
  610.9 46.0 %conditional.5 = (bf16[8,16,2048]{2,1,0:T(8,128)(2,1)S(1)}) conditional(s32[]{:T(128)} %clamp.14, (s32[8]{0:T(128)S(1)}, s32[]{:T(128)}, bf16[8,16,2048]{2,1,0:T(8,128)(2,1)S(1)}, f32[1,2048]{1,0:T(1,128)S(1)}, bf16[512,896]{1,0:T(8,128)(2,1)S(1)}, /*index=5*/bf16[512,896]{1,0:T(8,128)(2,1)}, ...), branch_computations={%region_17.19_spmd, %region_19.21_spmd, %region_21.23_spmd, %regio... | conditional | flops 11281891328 | bytes 92811184 | solution.py:385
  657.0 58.3 %conditional.6 = (bf16[8,16,2048]{2,1,0:T(8,128)(2,1)S(1)}) conditional(s32[]{:T(128)} %clamp.13, (s32[8]{0:T(128)S(1)}, s32[]{:T(128)}, bf16[8,16,2048]{2,1,0:T(8,128)(2,1)S(1)}, f32[1,2048]{1,0:T(1,128)S(1)}, bf16[512,896]{1,0:T(8,128)(2,1)S(1)}, /*index=5*/bf16[512,896]{1,0:T(8,128)(2,1)}, ...), branch_computations={%region_25.27_spmd, %region_27.29_spmd, %region_29.31_spmd, %regio... | conditional | flops 11281891328 | bytes 92811184 | solution.py:385
  659.7 10.7 %collective-permute-done.86 = bf16[2,16,2048]{2,1,0:T(8,128)(2,1)S(1)} collective-permute-done((bf16[2,16,2048]{2,1,0:T(8,128)(2,1)}, bf16[2,16,2048]{2,1,0:T(8,128)(2,1)S(1)}, u32[]{:S(2)}, u32[]{:S(2)}) %collective-permute-start.86) | collective-permute-done | bytes 131104 | tf_op jit(solution)/shard_map/cond/branch_0_fun/ppermute | solution.py:345
  715.3 62.9 %conditional.7 = (f32[8,4,32]{2,1,0:T(4,128)S(1)}) conditional(s32[]{:T(128)} %clamp.12, (s32[]{:T(128)}, s32[]{:T(128)}, s32[]{:T(128)}, s32[]{:T(128)}, s32[]{:T(128)}, /*index=5*/s32[]{:T(128)}, s32[]{:T(128)}, s32[]{:T(128)}, bf16[8,16,2048]{2,1,0:T(8,128)(2,1)S(1)}, f32[2048]{0:T(1024)S(1)}, ...), branch_computations={%region_33.35_spmd, %region_35.37_spmd, %region_37.39_spmd, %regio... | conditional | flops 33623498752 | bytes 64831668 | solution.py:432
  736.4 28.0 %head_stats.5 = f32[3,512]{1,0:T(4,128)} custom-call(bf16[64,2048]{1,0:T(8,128)(2,1)} %copy-done.52, bf16[64,2048]{1,0:T(8,128)(2,1)} %copy-done.148, bf16[64,2048]{1,0:T(8,128)(2,1)} %copy-done.147, bf16[64,2048]{1,0:T(8,128)(2,1)} %copy-done.146, bf16[64,2048]{1,0:T(8,128)(2,1)} %copy-done.145, bf16[64,2048]{1,0:T(8,128)(2,1)} %copy-done.172, ...), custom_call_target="tpu_custom_call" | custom-call | flops 16810770432 | bytes 34930688 | tf_op jit(solution)/shard_map/cond/branch_1_fun/head_stats/pallas_call | solution.py:210
  766.3 9.0 %all_gather.9 = f32[8,3,2,4,64]{4,3,2,1,0:T(4,128)S(1)} all-gather(f32[1,3,2,4,64]{4,3,2,1,0:T(4,128)S(1)} %copy.925), channel_id=1, replica_groups=mesh['section'=4,'vocab'=2,'dp'=4] {'section','vocab'}, dimensions={0}, use_global_device_ids=true | all-gather | bytes 55296 | tf_op jit(solution)/shard_map/cond/branch_1_fun/all_gather | solution.py:416
  (457 shorter events, 290.3 us)
Async XLA Ops:
  54.7 52.7 %collective-permute-start.226 = (bf16[512,896]{1,0:T(8,128)(2,1)}, bf16[512,896]{1,0:T(8,128)(2,1)}, u32[]{:S(2)}, u32[]{:S(2)}) collective-permute-start(bf16[512,896]{1,0:T(8,128)(2,1)} %get-tuple-element.1328), channel_id=1, source_target_pairs={{0,8},{8,0},{16,24},{24,16},{1,9},{9,1},{17,25},{25,17},{2,10},{10... | collective-permute-start | bytes 2752520 | tf_op jit(solution)/shard_map/ppermute | solution.py:29
  60.8 67.7 %collective-permute-start.225 = (bf16[512,896]{1,0:T(8,128)(2,1)}, bf16[512,896]{1,0:T(8,128)(2,1)}, u32[]{:S(2)}, u32[]{:S(2)}) collective-permute-start(bf16[512,896]{1,0:T(8,128)(2,1)} %get-tuple-element.1329), channel_id=1, source_target_pairs={{0,16},{8,24},{16,0},{24,8},{1,17},{9,25},{17,1},{25,9},{2,18},{10... | collective-permute-start | bytes 2752520 | tf_op jit(solution)/shard_map/ppermute | solution.py:29
  68.1 62.0 %collective-permute-start.224 = (bf16[512,896]{1,0:T(8,128)(2,1)S(1)}, bf16[512,896]{1,0:T(8,128)(2,1)}, u32[]{:S(2)}, u32[]{:S(2)}) collective-permute-start(bf16[512,896]{1,0:T(8,128)(2,1)S(1)} %get-tuple-element.1330), channel_id=1, source_target_pairs={{0,24},{8,16},{16,8},{24,0},{1,25},{9,17},{17,9},{25,1},{2,26},{10... | collective-permute-start | bytes 2752520 | tf_op jit(solution)/shard_map/ppermute | solution.py:29
  89.2 57.6 %collective-permute-start.232 = (bf16[896,512]{1,0:T(8,128)(2,1)}, bf16[896,512]{1,0:T(8,128)(2,1)}, u32[]{:S(2)}, u32[]{:S(2)}) collective-permute-start(bf16[896,512]{1,0:T(8,128)(2,1)} %get-tuple-element.1325), channel_id=1, source_target_pairs={{0,8},{8,0},{16,24},{24,16},{1,9},{9,1},{17,25},{25,17},{2,10},{10... | collective-permute-start | bytes 2752520 | tf_op jit(solution)/shard_map/ppermute | solution.py:29
  89.3 89.8 %collective-permute-start.231 = (bf16[896,512]{1,0:T(8,128)(2,1)S(1)}, bf16[896,512]{1,0:T(8,128)(2,1)}, u32[]{:S(2)}, u32[]{:S(2)}) collective-permute-start(bf16[896,512]{1,0:T(8,128)(2,1)S(1)} %get-tuple-element.1326), channel_id=1, source_target_pairs={{0,16},{8,24},{16,0},{24,8},{1,17},{9,25},{17,1},{25,9},{2,18},{10... | collective-permute-start | bytes 2752520 | tf_op jit(solution)/shard_map/ppermute | solution.py:29
  107.4 71.7 %collective-permute-start.213 = (bf16[128,2048]{1,0:T(8,128)(2,1)}, bf16[128,2048]{1,0:T(8,128)(2,1)}, u32[]{:S(2)}, u32[]{:S(2)}) collective-permute-start(bf16[128,2048]{1,0:T(8,128)(2,1)} %fusion.122.refs_1_), channel_id=1, source_target_pairs={{0,24},{8,16},{16,8},{24,0},{1,25},{9,17},{17,9},{25,1},{2,26},{10... | collective-permute-start | bytes 1572872 | tf_op jit(solution)/shard_map/ppermute | solution.py:29
  128.5 59.0 %collective-permute-start.212 = (bf16[128,2048]{1,0:T(8,128)(2,1)}, bf16[128,2048]{1,0:T(8,128)(2,1)}, u32[]{:S(2)}, u32[]{:S(2)}) collective-permute-start(bf16[128,2048]{1,0:T(8,128)(2,1)} %fusion.122.refs_1_), channel_id=1, source_target_pairs={{0,16},{8,24},{16,0},{24,8},{1,17},{9,25},{17,1},{25,9},{2,18},{10... | collective-permute-start | bytes 1572872 | tf_op jit(solution)/shard_map/ppermute | solution.py:29
  130.1 60.7 %collective-permute-start.230 = (bf16[896,512]{1,0:T(8,128)(2,1)S(1)}, bf16[896,512]{1,0:T(8,128)(2,1)S(1)}, u32[]{:S(2)}, u32[]{:S(2)}) collective-permute-start(bf16[896,512]{1,0:T(8,128)(2,1)S(1)} %get-tuple-element.1327), channel_id=1, source_target_pairs={{0,24},{8,16},{16,8},{24,0},{1,25},{9,17},{17,9},{25,1},{2,26},{10... | collective-permute-start | bytes 2752520 | tf_op jit(solution)/shard_map/ppermute | solution.py:29
  146.8 48.4 %collective-permute-start.214 = (bf16[128,2048]{1,0:T(8,128)(2,1)}, bf16[128,2048]{1,0:T(8,128)(2,1)S(1)}, u32[]{:S(2)}, u32[]{:S(2)}) collective-permute-start(bf16[128,2048]{1,0:T(8,128)(2,1)} %fusion.122.refs_1_), channel_id=1, source_target_pairs={{0,4},{4,0},{1,5},{5,1},{2,6},{6,2},{3,7},{7,3},{8,12},{12,8},{9,1... | collective-permute-start | bytes 1572872 | tf_op jit(solution)/shard_map/ppermute | solution.py:29
  199.1 55.2 %collective-permute-start.227 = (bf16[512,896]{1,0:T(8,128)(2,1)S(1)}, bf16[512,896]{1,0:T(8,128)(2,1)}, u32[]{:S(2)}, u32[]{:S(2)}) collective-permute-start(bf16[512,896]{1,0:T(8,128)(2,1)S(1)} %get-tuple-element.999), channel_id=1, source_target_pairs={{0,1},{3,2},{4,5},{7,6},{8,9},{11,10},{12,13},{15,14},{16,17},{19,... | collective-permute-start | bytes 2752520 | tf_op jit(solution)/shard_map/ppermute | solution.py:29
  205.1 68.9 %collective-permute-start.228 = (bf16[512,896]{1,0:T(8,128)(2,1)S(1)}, bf16[512,896]{1,0:T(8,128)(2,1)}, u32[]{:S(2)}, u32[]{:S(2)}) collective-permute-start(bf16[512,896]{1,0:T(8,128)(2,1)S(1)} %get-tuple-element.1000), channel_id=1, source_target_pairs={{0,2},{3,1},{4,6},{7,5},{8,10},{11,9},{12,14},{15,13},{16,18},{19,... | collective-permute-start | bytes 2752520 | tf_op jit(solution)/shard_map/ppermute | solution.py:29
  214.9 59.1 %collective-permute-start.229 = (bf16[512,896]{1,0:T(8,128)(2,1)S(1)}, bf16[512,896]{1,0:T(8,128)(2,1)}, u32[]{:S(2)}, u32[]{:S(2)}) collective-permute-start(bf16[512,896]{1,0:T(8,128)(2,1)S(1)} %get-tuple-element.1001), channel_id=1, source_target_pairs={{1,2},{2,1},{5,6},{6,5},{9,10},{10,9},{13,14},{14,13},{17,18},{18,... | collective-permute-start | bytes 2752520 | tf_op jit(solution)/shard_map/ppermute | solution.py:29
  234.6 59.0 %collective-permute-start.233 = (bf16[896,512]{1,0:T(8,128)(2,1)S(1)}, bf16[896,512]{1,0:T(8,128)(2,1)}, u32[]{:S(2)}, u32[]{:S(2)}) collective-permute-start(bf16[896,512]{1,0:T(8,128)(2,1)S(1)} %get-tuple-element.1002), channel_id=1, source_target_pairs={{0,1},{3,2},{4,5},{7,6},{8,9},{11,10},{12,13},{15,14},{16,17},{19,... | collective-permute-start | bytes 2752520 | tf_op jit(solution)/shard_map/ppermute | solution.py:29
  241.1 71.9 %collective-permute-start.234 = (bf16[896,512]{1,0:T(8,128)(2,1)S(1)}, bf16[896,512]{1,0:T(8,128)(2,1)}, u32[]{:S(2)}, u32[]{:S(2)}) collective-permute-start(bf16[896,512]{1,0:T(8,128)(2,1)S(1)} %get-tuple-element.1003), channel_id=1, source_target_pairs={{0,2},{3,1},{4,6},{7,5},{8,10},{11,9},{12,14},{15,13},{16,18},{19,... | collective-permute-start | bytes 2752520 | tf_op jit(solution)/shard_map/ppermute | solution.py:29
  254.3 58.6 %collective-permute-start.235 = (bf16[896,512]{1,0:T(8,128)(2,1)S(1)}, bf16[896,512]{1,0:T(8,128)(2,1)}, u32[]{:S(2)}, u32[]{:S(2)}) collective-permute-start(bf16[896,512]{1,0:T(8,128)(2,1)S(1)} %get-tuple-element.1004), channel_id=1, source_target_pairs={{1,2},{2,1},{5,6},{6,5},{9,10},{10,9},{13,14},{14,13},{17,18},{18,... | collective-permute-start | bytes 2752520 | tf_op jit(solution)/shard_map/ppermute | solution.py:29
  366.7 64.9 %collective-permute-start.247 = (bf16[8,128]{1,0:T(8,128)(2,1)S(1)}, bf16[8,128]{1,0:T(8,128)(2,1)S(1)}, u32[]{:S(2)}, u32[]{:S(2)}) collective-permute-start(bf16[8,128]{1,0:T(8,128)(2,1)S(1)} %fusion.150), channel_id=1, source_target_pairs={{1,0},{2,3},{5,4},{6,7},{9,8},{10,11},{13,12},{14,15},{17,16},{18,... | collective-permute-start | bytes 6152 | tf_op jit(solution)/shard_map/ppermute | solution.py:366
  420.0 92.7 %collective-permute-start.244 = (bf16[512,896]{1,0:T(8,128)(2,1)}, bf16[512,896]{1,0:T(8,128)(2,1)}, u32[]{:S(2)}, u32[]{:S(2)}) collective-permute-start(bf16[512,896]{1,0:T(8,128)(2,1)} %copy-done.30), channel_id=1, source_target_pairs={{1,0},{2,3},{5,4},{6,7},{9,8},{10,11},{13,12},{14,15},{17,16},{18,... | collective-permute-start | bytes 2752520 | tf_op jit(solution)/shard_map/ppermute | solution.py:29
  421.3 95.6 %collective-permute-start.245 = (bf16[512,896]{1,0:T(8,128)(2,1)}, bf16[512,896]{1,0:T(8,128)(2,1)}, u32[]{:S(2)}, u32[]{:S(2)}) collective-permute-start(bf16[512,896]{1,0:T(8,128)(2,1)} %copy-done.29), channel_id=1, source_target_pairs={{1,3},{2,0},{5,7},{6,4},{9,11},{10,8},{13,15},{14,12},{17,19},{18,... | collective-permute-start | bytes 2752520 | tf_op jit(solution)/shard_map/ppermute | solution.py:29
  422.6 95.6 %collective-permute-start.246 = (bf16[512,896]{1,0:T(8,128)(2,1)}, bf16[512,896]{1,0:T(8,128)(2,1)}, u32[]{:S(2)}, u32[]{:S(2)}) collective-permute-start(bf16[512,896]{1,0:T(8,128)(2,1)} %copy-done.27), channel_id=1, source_target_pairs={{0,3},{3,0},{4,7},{7,4},{8,11},{11,8},{12,15},{15,12},{16,19},{19,... | collective-permute-start | bytes 2752520 | tf_op jit(solution)/shard_map/ppermute | solution.py:29
  431.6 140.0 %collective-permute-start.248 = (bf16[512,896]{1,0:T(8,128)(2,1)}, bf16[512,896]{1,0:T(8,128)(2,1)}, u32[]{:S(2)}, u32[]{:S(2)}) collective-permute-start(bf16[512,896]{1,0:T(8,128)(2,1)} %copy-done.28), channel_id=1, source_target_pairs={{1,0},{2,3},{5,4},{6,7},{9,8},{10,11},{13,12},{14,15},{17,16},{18,... | collective-permute-start | bytes 2752520 | tf_op jit(solution)/shard_map/ppermute | solution.py:29
  432.9 149.8 %collective-permute-start.249 = (bf16[512,896]{1,0:T(8,128)(2,1)}, bf16[512,896]{1,0:T(8,128)(2,1)}, u32[]{:S(2)}, u32[]{:S(2)}) collective-permute-start(bf16[512,896]{1,0:T(8,128)(2,1)} %copy-done.23), channel_id=1, source_target_pairs={{1,3},{2,0},{5,7},{6,4},{9,11},{10,8},{13,15},{14,12},{17,19},{18,... | collective-permute-start | bytes 2752520 | tf_op jit(solution)/shard_map/ppermute | solution.py:29
  512.7 70.1 %collective-permute-start.250 = (bf16[512,896]{1,0:T(8,128)(2,1)}, bf16[512,896]{1,0:T(8,128)(2,1)}, u32[]{:S(2)}, u32[]{:S(2)}) collective-permute-start(bf16[512,896]{1,0:T(8,128)(2,1)} %copy-done.22), channel_id=1, source_target_pairs={{0,3},{3,0},{4,7},{7,4},{8,11},{11,8},{12,15},{15,12},{16,19},{19,... | collective-permute-start | bytes 2752520 | tf_op jit(solution)/shard_map/ppermute | solution.py:29
  516.9 94.0 %collective-permute-start.251 = (bf16[896,512]{1,0:T(8,128)(2,1)}, bf16[896,512]{1,0:T(8,128)(2,1)}, u32[]{:S(2)}, u32[]{:S(2)}) collective-permute-start(bf16[896,512]{1,0:T(8,128)(2,1)} %copy-done.26), channel_id=1, source_target_pairs={{1,0},{2,3},{5,4},{6,7},{9,8},{10,11},{13,12},{14,15},{17,16},{18,... | collective-permute-start | bytes 2752520 | tf_op jit(solution)/shard_map/ppermute | solution.py:29
  518.3 92.7 %collective-permute-start.252 = (bf16[896,512]{1,0:T(8,128)(2,1)}, bf16[896,512]{1,0:T(8,128)(2,1)}, u32[]{:S(2)}, u32[]{:S(2)}) collective-permute-start(bf16[896,512]{1,0:T(8,128)(2,1)} %copy-done.25), channel_id=1, source_target_pairs={{1,3},{2,0},{5,7},{6,4},{9,11},{10,8},{13,15},{14,12},{17,19},{18,... | collective-permute-start | bytes 2752520 | tf_op jit(solution)/shard_map/ppermute | solution.py:29
  (143 other events, 2035.6 us)
where the time goes:
time: 799 us; the launch traced here: 790 us
  waiting for transfers between devices  466 us (58%)
  starting transfers between devices  116 us (15%)
  Pallas kernels  79.8 us (10%)
  other arithmetic  35.9 us (4%)
  local copies, waits for them, and re-layouts  32.8 us (4%)
  between operations  26.1 us (3%)
  loops' own time  24.3 us (3%)
  blocking collectives  9.04 us (1%)
    ppermute x98, waiting for transfers between devices, swapped(): return lax.ppermute(block, axis, pairs)  450 us
    ppermute x98, starting transfers between devices, swapped(): return lax.ppermute(block, axis, pairs)  107 us
    pallas_call x4, Pallas kernels, layer_products(): pl.pallas_call(lambda *refs: layer_body(*refs, pieces=pieces, blocks=bloc...  51.8 us
    pallas_call x1, Pallas kernels, head_stats(): pl.pallas_call(lambda *refs: head_body(*refs, pieces=pieces, columns=colu...  28 us
    another operation x3, loops' own time, planes_step(): state = lax.switch(which, [branch_of(n) for n in sizes], state, weights)  17.5 us
  transfers between devices with their start and end apart: 103, of which 50 were waited for; matrix products, arithmetic and copies ran while one was open for 6% of the time, Pallas kernels for 2%

commit v1 on v0

--- a/solution.py
+++ b/solution.py
@@ -51,14 +51,14 @@
     return lax.optimization_barrier((value,) + others)[0]
 
 
-def layer_body(plane, *refs, pieces, blocks, steps):
+def layer_body(plane, *refs, pieces, blocks, steps, turned):
     rows, refs = refs[:pieces], refs[pieces:]
     gates, ups, downs = refs[:blocks], refs[blocks : 2 * blocks], refs[2 * blocks : 3 * blocks]
     refs = refs[3 * blocks :]
     kept, sent = refs[: pieces // 2], refs[pieces // 2 : pieces]
     gathered, total = refs[pieces:]
     each = rows[0].shape[0]
-    features = gates[0].shape[0]
+    features = downs[0].shape[1]
     step = pl.program_id(0)
 
     def place(mask):
@@ -82,7 +82,12 @@
             result = None
             for mask in range(blocks):
                 here = gathered[pl.ds(first, tile), mask * features : (mask + 1) * features]
-                part = jnp.dot(here, matrices[mask][...], preferred_element_type=jnp.float32)
+                part = lax.dot_general(
+                    here,
+                    matrices[mask][...],
+                    (((1,), (1 if turned else 0,)), ((), ())),
+                    preferred_element_type=jnp.float32,
+                )
                 result = part if result is None else result + part
             return result
 
@@ -116,21 +121,28 @@
                     sent[i - pieces // 2][:, place(mask)] = block.astype(jnp.bfloat16)
 
 
-def layer_products(rows, weights, plane):
+def layer_products(rows, weights, plane, part_of=None):
     gates, ups, downs = weights
     pieces, blocks = len(rows), len(gates)
     each, width = rows[0].shape
-    features, hidden = gates[0].shape
-    steps = 2 if hidden % 256 == 0 else 1
+    hidden, features = downs[0].shape
+    turned = part_of is not None
+    steps = 2 if hidden % 256 == 0 and not turned else 1
     part = hidden // steps
+    if turned:
+        across_hidden = pl.BlockSpec((hidden, features), lambda i, plane: (0, part_of))
+    else:
+        across_hidden = pl.BlockSpec((features, part), lambda i, plane: (0, i))
     whole = pl.BlockSpec((each, width), lambda i, plane: (0, 0))
     results = pl.pallas_call(
-        lambda *refs: layer_body(*refs, pieces=pieces, blocks=blocks, steps=steps),
+        lambda *refs: layer_body(
+            *refs, pieces=pieces, blocks=blocks, steps=steps, turned=turned
+        ),
         grid_spec=pltpu.PrefetchScalarGridSpec(
             num_scalar_prefetch=1,
             grid=(steps,),
             in_specs=[whole] * pieces
-            + [pl.BlockSpec((features, part), lambda i, plane: (0, i))] * (2 * blocks)
+            + [across_hidden] * (2 * blocks)
             + [pl.BlockSpec((part, features), lambda i, plane: (i, 0))] * blocks,
             out_specs=[whole] * pieces,
             scratch_shapes=[
@@ -153,7 +165,7 @@
     return results[: pieces // 2], results[pieces // 2 :]
 
 
-def head_body(*refs, pieces, columns, tile, lines):
+def head_body(*refs, pieces, columns, tile, portion, lines):
     rows = refs[:pieces]
     labels, weight = refs[pieces : pieces + 2]
     stats_out = refs[pieces + 2]
@@ -175,22 +187,20 @@
     some = min(count, 256)
     for first in range(0, count, some):
         span = slice(first, first + some)
-        logits = jnp.dot(weight[...], turned[:, span], preferred_element_type=jnp.float32)
-        place = step * tile + lax.broadcasted_iota(jnp.int32, (tile, some), 0)
-        found = jnp.where(place == labels[:, span], logits, 0.0)
-        logits = jnp.where(place < columns, logits, -1e30)
-        groups = [slice(i * lines, (i + 1) * lines) for i in range(tile // lines)]
-        highest = peak[:, span]
-        gained = picked[:, span]
-        for group in groups:
-            highest = jnp.maximum(highest, logits[group])
-            gained = gained + found[group]
-        sums = total[:, span] * jnp.exp(peak[:, span] - highest)
-        for group in groups:
-            sums = sums + jnp.exp(logits[group] - highest)
-        peak[:, span] = highest
-        total[:, span] = sums
-        picked[:, span] = gained
+        for part in range(0, tile, portion):
+            logits = jnp.dot(
+                weight[part : part + portion, :], turned[:, span], preferred_element_type=jnp.float32
+            )
+            place = step * tile + part + lax.broadcasted_iota(jnp.int32, (portion, some), 0)
+            found = jnp.where(place == labels[:, span], logits, 0.0)
+            logits = jnp.where(place < columns, logits, -1e30)
+            grouped = logits.reshape(portion // lines, lines, some)
+            before = peak[:, span]
+            highest = jnp.maximum(before, jnp.max(grouped, axis=0))
+            sums = jnp.sum(jnp.exp(grouped - highest[None]), axis=0)
+            peak[:, span] = highest
+            total[:, span] = total[:, span] * jnp.exp(before - highest) + sums
+            picked[:, span] += jnp.sum(found.reshape(portion // lines, lines, some), axis=0)
 
     @pl.when(step == steps - 1)
     def _():
@@ -204,11 +214,13 @@
     pieces = len(rows)
     each, width = rows[0].shape
     columns = weight.shape[0]
-    tile, lines = 512, 8
+    tile, portion, lines = 1024, 256, 8
     count = pieces * each
     whole = pl.BlockSpec((each, width), lambda i: (0, 0))
     return pl.pallas_call(
-        lambda *refs: head_body(*refs, pieces=pieces, columns=columns, tile=tile, lines=lines),
+        lambda *refs: head_body(
+            *refs, pieces=pieces, columns=columns, tile=tile, portion=portion, lines=lines
+        ),
         grid=(pl.cdiv(columns, tile),),
         in_specs=[whole] * pieces
         + [
@@ -270,9 +282,9 @@
             return lax.dynamic_slice_in_dim(matrix[0], column * hidden_each, hidden_each, 0)
         return lax.dynamic_slice_in_dim(matrix[0], column * hidden_each, hidden_each, 1)
 
-    def across(matrix):
+    def across(matrix, *earlier):
         return [
-            swapped(column_block(matrix, my_column ^ mask), "section", mask)
+            swapped(after(column_block(matrix, my_column ^ mask), *earlier), "section", mask)
             if mask
             else column_block(matrix, my_column)
             for mask in range(sections)
@@ -286,6 +298,14 @@
 
     def blocks_for(held):
         return [chosen(held, layer_at(my_plane ^ mask) ^ my_column) for mask in range(sections)]
+
+    def halves_for(held, layer, axis):
+        block = chosen(held, layer ^ my_column)
+        first, second = jnp.split(block, 2, axis)
+        return [
+            jnp.where((my_plane ^ mask) == early_planes[0], first, second)
+            for mask in range(sections)
+        ]
 
     def towards(blocks, planes, *earlier):
         return [
@@ -293,20 +313,39 @@
             for mask in range(sections)
         ]
 
+    def both_halves(held, axis):
+        return [halves_for(held, layer, axis) for layer in range(2)]
+
+    def stacked(halves):
+        return [jnp.concatenate(pair, 0) for pair in zip(*halves)]
+
+    gains = [norm_gain] + [swapped(norm_gain, "section", mask) for mask in range(1, sections)]
+
+    def gain_of(layer, *earlier):
+        held = lax.optimization_barrier((tuple(gains), earlier))[0]
+        return chosen(held, layer ^ my_column)
+
     gates = across(w_gate)
-    ups = across(w_up)
-    downs = across(w_down)
-    gates = blocks_for(gates)
-    gates_early = towards(gates, early_planes)
-    ups = blocks_for(ups)
-    ups_early = towards(ups, early_planes)
-    downs = blocks_for(downs)
-    downs_early = towards(downs, early_planes)
-    gates_late = towards(gates, late_planes, *downs_early[1:])
-    early = (gates_early, ups_early, downs_early)
-
-    gains = [norm_gain] + [swapped(norm_gain, "section", mask) for mask in range(1, sections)]
-    my_gain = chosen(gains, my_layer ^ my_column)
+    gate_halves = stacked(both_halves(gates, 1))
+    ups = across(w_up, *gates[1:])
+    gates_early = towards(gate_halves, early_planes)
+    gain_first = gain_of(0, *gate_halves)
+    ups = lax.optimization_barrier((ups, gate_halves))[0]
+    up_halves = stacked(both_halves(ups, 1))
+    downs = across(w_down, *ups[1:])
+    ups_early = towards(up_halves, early_planes)
+    gain_second = gain_of(1, *up_halves)
+    downs = lax.optimization_barrier((downs, up_halves))[0]
+    downs_early = []
+    for halves in both_halves(downs, 0):
+        downs_early.append(towards(halves, early_planes))
+    gates, ups, downs = blocks_for(gates), blocks_for(ups), blocks_for(downs)
+    gates_late = towards(gates, late_planes, *downs_early[0][1:])
+    gates_early, ups_early = [block.T for block in gates_early], [block.T for block in ups_early]
+    early = [(gates_early, ups_early, downs_early[layer]) for layer in range(2)]
+
+    layer_gains = [gain_first, gain_second]
+    layer_gains += [chosen(gains, my_layer ^ my_column)] * (layers - 2)
     labels_by = [targets[:, 0]] + [
         swapped(targets[:, 0], "dp", mask) for mask in range(1, sections)
     ]
@@ -327,8 +366,12 @@
 
     def run_layer(layer, state, weights, count):
         current = state[:count].reshape(count * rows_each, width)
-        rows = spread_rows(rms_scaled(current, my_gain).astype(jnp.bfloat16))
-        branch = collected(*layer_products(rows, weights, my_plane[None]))
+        rows = spread_rows(rms_scaled(current, layer_gains[layer]).astype(jnp.bfloat16))
+        branch = collected(*layer_products(rows, weights, my_plane[None], layer if layer < 2 else 0))
+        if layer < 2:
+            mine = branch.astype(jnp.bfloat16)
+            other = swapped(mine, "dp", early_planes[0] ^ early_planes[1], early_planes)
+            branch = mine.astype(jnp.float32) + other.astype(jnp.float32)
         moved = (current.astype(jnp.float32) + branch).astype(jnp.bfloat16)
         keep = (sorted_depths[:count] > layer)[:, None, None]
         moved = jnp.where(keep, moved.reshape(count, rows_each, width), state[:count])
@@ -350,12 +393,17 @@
     sorted_rows = jnp.concatenate(
         [lax.dynamic_slice_in_dim(entering[:, 0], order[i], 1, 0) for i in range(micro_count)], 0
     )
-    pairs = [
-        (linear(s, c, s), linear(s, c, plane_of[0])) for s in range(sections) for c in range(cores)
+    sorted_rows = after(sorted_rows, labels_all)
+    arrivals = [
+        lax.ppermute(
+            sorted_rows,
+            MESH_AXES,
+            [(linear(s, c, s), linear(s, c, plane)) for s in range(sections) for c in range(cores)],
+        )
+        for plane in early_planes
     ]
-    state = lax.ppermute(after(sorted_rows, labels_all), MESH_AXES, pairs)
-    state = run_layer(0, state, early, micro_count)
-    state = handed_on(state, 1, micro_count)
+    state = jnp.where(my_plane == early_planes[0], arrivals[0], arrivals[1])
+    state = run_layer(0, state, early[0], micro_count)
     word = state[0, :8, :128].astype(jnp.float32)
     pairs = [
         (linear(s, c, source), linear(s, c, source ^ 1))
@@ -366,12 +414,12 @@
     word = lax.ppermute(word, MESH_AXES, pairs)
     ups_late = towards(ups, late_planes, state, word)
     downs_late = towards(downs, late_planes, state, word)
-    late_blocks = (gates_late, ups_late, downs_late)
+    late_blocks = ([b.T for b in gates_late], [b.T for b in ups_late], downs_late)
     sizes = [n for n in range(2, micro_count + 1, 2)]
     for layer in range(1, layers):
         if layer == 2:
             state, late_blocks = lax.optimization_barrier((state, late_blocks))
-        weights = early if layer < 2 else late_blocks
+        weights = early[1] if layer < 2 else late_blocks
 
         def branch_of(count, layer=layer):
             def run(state, weights):

time: 799 us -> 792 us (level)
  waiting for transfers between devices: 466 us -> 395 us
  starting transfers between devices: 116 us -> 156 us
  local copies, waits for them, and re-layouts: 32.8 us -> 48.2 us
  loops' own time: 24.3 us -> 38.6 us
  Pallas kernels: 79.8 us -> 67.2 us
    ppermute x98 -> x103, waiting for transfers between devices: 450 us -> 388 us  [swapped(): return lax.ppermute(block, axis, pairs)]
    ppermute x98 -> x103, starting transfers between devices: 107 us -> 143 us  [swapped(): return lax.ppermute(block, axis, pairs)]
    dynamic_slice x2 -> x9, local copies, waits for them, and re-layouts: 4.86 us -> 19.8 us  [column_block(): lax.dynamic_slice_in_dim(matrix[0], column * hidden_each, hidden_each, 1)]
    another operation x1, loops' own time: 6.78 us -> 20.5 us  [planes_step(): table = lax.switch(which, [head(n) for n in sizes], state, head_weight.T)]
    pallas_call x4, Pallas kernels: 51.8 us -> 40.3 us  [layer_products(): pl.pallas_call(lambda *refs: layer_body(*refs, pieces=pieces, blocks=bloc...]
  transfers between devices with their start and end apart: 103 -> 108, of which waited for: 50 -> 46; matrix products, arithmetic and copies ran while one was open for 6% -> 9% of each run, Pallas kernels for 2% -> 1%
where the time goes in v1:
time: 792 us; the launch traced here: 783 us
  waiting for transfers between devices  395 us (50%)
  starting transfers between devices  156 us (20%)
  Pallas kernels  67.2 us (8%)
  local copies, waits for them, and re-layouts  48.2 us (6%)
  other arithmetic  43.7 us (6%)
  loops' own time  38.6 us (5%)
  between operations  25.5 us (3%)
  blocking collectives  9.02 us (1%)
    ppermute x103, waiting for transfers between devices, swapped(): return lax.ppermute(block, axis, pairs)  388 us
    ppermute x103, starting transfers between devices, swapped(): return lax.ppermute(block, axis, pairs)  143 us
    pallas_call x4, Pallas kernels, layer_products(): pl.pallas_call(lambda *refs: layer_body(*refs, pieces=pieces, blocks=bloc...  40.3 us
    pallas_call x1, Pallas kernels, head_stats(): pl.pallas_call(lambda *refs: head_body(*refs, pieces=pieces, columns=colu...  26.9 us
    another operation x1, loops' own time, planes_step(): table = lax.switch(which, [head(n) for n in sizes], state, head_weight.T)  20.5 us
    dynamic_slice x9, local copies, waits for them, and re-layouts, column_block(): lax.dynamic_slice_in_dim(matrix[0], column * hidden_each, hidden_each, 1)  19.8 us
    another operation x3, loops' own time, planes_step(): state = lax.switch(which, [branch_of(n) for n in sizes], state, weights)  18.1 us
  transfers between devices with their start and end apart: 108, of which 46 were waited for; matrix products, arithmetic and copies ran while one was open for 9% of the time, Pallas kernels for 1%

profile of v1, /device:TPU:0, one launch (start us, length us, event | category | flops | bytes accessed | tf_op | source)
XLA Modules:
  0.0 783.0 jit_solution(10928913556956137516)
XLA Ops:
  68.9 23.7 %collective-permute-done.217 = bf16[512,896]{0,1:T(8,128)(2,1)S(1)} collective-permute-done((bf16[512,896]{0,1:T(8,128)(2,1)}, bf16[512,896]{0,1:T(8,128)(2,1)S(1)}, u32[]{:S(2)}, u32[]{:S(2)}) %collective-permute-start.217) | collective-permute-done | bytes 917536 | tf_op jit(solution)/shard_map/ppermute | solution.py:29
  119.2 27.2 %collective-permute-done.230 = bf16[512,896]{0,1:T(8,128)(2,1)} collective-permute-done((bf16[512,896]{0,1:T(8,128)(2,1)}, bf16[512,896]{0,1:T(8,128)(2,1)}, u32[]{:S(2)}, u32[]{:S(2)}) %collective-permute-start.230) | collective-permute-done | bytes 917536 | tf_op jit(solution)/shard_map/ppermute | solution.py:29
  168.5 14.3 %collective-permute-done.235 = bf16[896,512]{1,0:T(8,128)(2,1)S(1)} collective-permute-done((bf16[896,512]{1,0:T(8,128)(2,1)S(1)}, bf16[896,512]{1,0:T(8,128)(2,1)S(1)}, u32[]{:S(2)}, u32[]{:S(2)}) %collective-permute-start.235) | collective-permute-done | bytes 917536 | tf_op jit(solution)/shard_map/ppermute | solution.py:29
  184.1 12.7 %collective-permute-done.237 = bf16[896,512]{1,0:T(8,128)(2,1)S(1)} collective-permute-done((bf16[896,512]{1,0:T(8,128)(2,1)S(1)}, bf16[896,512]{1,0:T(8,128)(2,1)S(1)}, u32[]{:S(2)}, u32[]{:S(2)}) %collective-permute-start.237) | collective-permute-done | bytes 917536 | tf_op jit(solution)/shard_map/ppermute | solution.py:29
  206.7 15.1 %collective-permute-start.233 = (bf16[1024,448]{0,1:T(8,128)(2,1)S(1)}, bf16[1024,448]{0,1:T(8,128)(2,1)}, u32[]{:S(2)}, u32[]{:S(2)}) collective-permute-start(bf16[1024,448]{0,1:T(8,128)(2,1)S(1)} %pad_maximum_fusion.15), channel_id=1, source_target_pairs={{0,2},{3,1},{4,6},{7,5},{8,10},{11,9},{12,14},{15,13},{16,18},{19,... | collective-permute-start | bytes 2752520 | tf_op jit(solution)/shard_map/ppermute | solution.py:29
  231.6 12.8 %collective-permute-done.233 = bf16[1024,448]{0,1:T(8,128)(2,1)} collective-permute-done((bf16[1024,448]{0,1:T(8,128)(2,1)S(1)}, bf16[1024,448]{0,1:T(8,128)(2,1)}, u32[]{:S(2)}, u32[]{:S(2)}) %collective-permute-start.233) | collective-permute-done | bytes 917536 | tf_op jit(solution)/shard_map/ppermute | solution.py:29
  244.4 9.8 %collective-permute-done.239.refs_19_ = bf16[448,512]{1,0:T(8,128)(2,1)S(1)} collective-permute-done((bf16[448,512]{1,0:T(8,128)(2,1)S(1)}, bf16[448,512]{1,0:T(8,128)(2,1)S(1)}, u32[]{:S(2)}, u32[]{:S(2)}) %collective-permute-start.239) | collective-permute-done | bytes 458784 | tf_op jit(solution)/shard_map/ppermute | solution.py:29
  254.2 9.4 %collective-permute-done.238.refs_18_ = bf16[448,512]{1,0:T(8,128)(2,1)S(1)} collective-permute-done((bf16[448,512]{1,0:T(8,128)(2,1)S(1)}, bf16[448,512]{1,0:T(8,128)(2,1)S(1)}, u32[]{:S(2)}, u32[]{:S(2)}) %collective-permute-start.238) | collective-permute-done | bytes 458784 | tf_op jit(solution)/shard_map/ppermute | solution.py:29
  264.3 14.8 %layer_products.25 = (f32[128,2048]{1,0:T(8,128)}, f32[128,2048]{1,0:T(8,128)}, f32[128,2048]{1,0:T(8,128)}, f32[128,2048]{1,0:T(8,128)}, bf16[128,2048]{1,0:T(8...) custom-call(s32[1]{0:T(128)} %bitcast.114.refs_0_, ...), custom_call_target="tpu_custom_call" | custom-call | flops 5637144576 | bytes 15990784 | tf_op jit(solution)/shard_map/layer_products/pallas_call | solution.py:137
  290.3 9.2 %collective-permute-done.242 = bf16[128,2048]{1,0:T(8,128)(2,1)S(1)} collective-permute-done((bf16[128,2048]{1,0:T(8,128)(2,1)}, bf16[128,2048]{1,0:T(8,128)(2,1)S(1)}, u32[]{:S(2)}, u32[]{:S(2)}) %collective-permute-start.242) | collective-permute-done | bytes 524320 | tf_op jit(solution)/shard_map/ppermute | solution.py:29
  299.5 10.5 %collective-permute-done.244 = bf16[128,2048]{1,0:T(8,128)(2,1)} collective-permute-done((bf16[128,2048]{1,0:T(8,128)(2,1)}, bf16[128,2048]{1,0:T(8,128)(2,1)}, u32[]{:S(2)}, u32[]{:S(2)}) %collective-permute-start.244) | collective-permute-done | bytes 524320 | tf_op jit(solution)/shard_map/ppermute | solution.py:29
  315.0 21.6 %collective-permute-start.250 = (bf16[448,512]{1,0:T(8,128)(2,1)S(1)}, bf16[448,512]{1,0:T(8,128)(2,1)}, u32[]{:S(2)}, u32[]{:S(2)}) collective-permute-start(bf16[448,512]{1,0:T(8,128)(2,1)S(1)} %get-tuple-element.1387), channel_id=1, source_target_pairs={{0,2},{3,1},{4,6},{7,5},{8,10},{11,9},{12,14},{15,13},{16,18},{19,... | collective-permute-start | bytes 1376264 | tf_op jit(solution)/shard_map/ppermute | solution.py:29
  346.8 8.6 %collective-permute-done.249 = bf16[448,512]{1,0:T(8,128)(2,1)} collective-permute-done((bf16[448,512]{1,0:T(8,128)(2,1)S(1)}, bf16[448,512]{1,0:T(8,128)(2,1)}, u32[]{:S(2)}, u32[]{:S(2)}) %collective-permute-start.249) | collective-permute-done | bytes 458784 | tf_op jit(solution)/shard_map/ppermute | solution.py:29
  355.4 45.1 %conditional.4 = (bf16[8,16,2048]{2,1,0:T(8,128)(2,1)S(1)}) conditional(s32[]{:T(128)} %clamp.15, (s32[8]{0:T(128)S(1)}, bf16[8,16,2048]{2,1,0:T(8,128)(2,1)S(1)}, s32[]{:T(128)}, f32[1,2048]{1,0:T(1,128)S(1)}, bf16[448,1024]{1,0:T(8,128)(2,1)}, /*index=5*/bf16[448,1024]{1,0:T(8,128)(2,1)}, ...), branch_computations={%region_9.11_spmd, %region_11.13_spmd, %region_13.15_spmd, %region... | conditional | flops 5645533184 | bytes 92024776 | solution.py:433
  372.2 8.8 %layer_products.14 = (f32[64,2048]{1,0:T(8,128)}, f32[64,2048]{1,0:T(8,128)}, f32[64,2048]{1,0:T(8,128)}, f32[64,2048]{1,0:T(8,128)}, bf16[64,2048]{1,0:T(8,128)...) custom-call(s32[1]{0:T(128)} %bitcast.5.refs_0_, ...), custom_call_target="tpu_custom_call" | custom-call | flops 2818572288 | bytes 10747904 | tf_op jit(solution)/shard_map/cond/branch_1_fun/layer_products/pallas_call | solution.py:137
  409.1 89.3 %collective-permute-done.252 = bf16[512,896]{0,1:T(8,128)(2,1)} collective-permute-done((bf16[512,896]{0,1:T(8,128)(2,1)}, bf16[512,896]{0,1:T(8,128)(2,1)}, u32[]{:S(2)}, u32[]{:S(2)}) %collective-permute-start.252) | collective-permute-done | bytes 917536 | tf_op jit(solution)/shard_map/ppermute | solution.py:29
  504.4 53.0 %collective-permute-done.256 = bf16[512,896]{0,1:T(8,128)(2,1)} collective-permute-done((bf16[512,896]{0,1:T(8,128)(2,1)}, bf16[512,896]{0,1:T(8,128)(2,1)}, u32[]{:S(2)}, u32[]{:S(2)}) %collective-permute-start.256) | collective-permute-done | bytes 917536 | tf_op jit(solution)/shard_map/ppermute | solution.py:29
  567.6 28.4 %collective-permute-done.259 = bf16[896,512]{1,0:T(8,128)(2,1)} collective-permute-done((bf16[896,512]{1,0:T(8,128)(2,1)}, bf16[896,512]{1,0:T(8,128)(2,1)}, u32[]{:S(2)}, u32[]{:S(2)}) %collective-permute-start.259) | collective-permute-done | bytes 917536 | tf_op jit(solution)/shard_map/ppermute | solution.py:29
  596.1 45.0 %conditional.5 = (bf16[8,16,2048]{2,1,0:T(8,128)(2,1)S(1)}) conditional(s32[]{:T(128)} %clamp.14, (s32[8]{0:T(128)S(1)}, s32[]{:T(128)}, bf16[8,16,2048]{2,1,0:T(8,128)(2,1)S(1)}, f32[1,2048]{1,0:T(1,128)S(1)}, bf16[896,512]{1,0:T(8,128)(2,1)S(1)}, /*index=5*/bf16[896,512]{1,0:T(8,128)(2,1)}, ...), branch_computations={%region_17.19_spmd, %region_19.21_spmd, %region_21.23_spmd, %regio... | conditional | flops 11281891328 | bytes 97005520 | solution.py:433
  641.1 54.3 %conditional.6 = (bf16[8,16,2048]{2,1,0:T(8,128)(2,1)S(1)}) conditional(s32[]{:T(128)} %clamp.13, (s32[8]{0:T(128)}, s32[]{:T(128)}, bf16[8,16,2048]{2,1,0:T(8,128)(2,1)S(1)}, f32[1,2048]{1,0:T(1,128)S(1)}, bf16[896,512]{1,0:T(8,128)(2,1)S(1)}, /*index=5*/bf16[896,512]{1,0:T(8,128)(2,1)}, bf16[896,512]{1,0:T(8,128)(2,1)}, ...), branch_computations={%region_25.27_spmd, %region_27.29_spmd, %region_29.31_spmd, %regio... | conditional | flops 11281891328 | bytes 97005680 | solution.py:433
  666.0 8.4 %layer_products.21 = (f32[32,2048]{1,0:T(8,128)}, f32[32,2048]{1,0:T(8,128)}, f32[32,2048]{1,0:T(8,128)}, f32[32,2048]{1,0:T(8,128)}, bf16[32,2048]{1,0:T(8,128)...) custom-call(s32[1]{0:T(128)} %bitcast.33.refs_0_, ...), custom_call_target="tpu_custom_call" | custom-call | flops 2818572288 | bytes 13631488 | tf_op jit(solution)/shard_map/cond/branch_0_fun/layer_products/pallas_call | solution.py:137
  695.5 75.7 %conditional.7 = (f32[8,4,32]{2,1,0:T(4,128)S(1)}) conditional(s32[]{:T(128)} %clamp.12, (s32[]{:T(128)}, s32[]{:T(128)}, s32[]{:T(128)}, s32[]{:T(128)}, s32[]{:T(128)}, /*index=5*/s32[]{:T(128)}, s32[]{:T(128)}, s32[]{:T(128)}, bf16[8,16,2048]{2,1,0:T(8,128)(2,1)S(1)}, f32[2048]{0:T(1024)S(1)}, ...), branch_computations={%region_33.35_spmd, %region_35.37_spmd, %region_37.39_spmd, %regio... | conditional | flops 33623498752 | bytes 64848084 | solution.py:480
  724.1 26.9 %head_stats.5 = f32[3,512]{1,0:T(4,128)} custom-call(bf16[64,2048]{1,0:T(8,128)(2,1)} %copy-done.84, bf16[64,2048]{1,0:T(8,128)(2,1)} %copy-done.188, bf16[64,2048]{1,0:T(8,128)(2,1)} %copy-done.187, bf16[64,2048]{1,0:T(8,128)(2,1)} %copy-done.186, bf16[64,2048]{1,0:T(8,128)(2,1)} %copy-done.185, bf16[64,2048]{1,0:T(8,128)(2,1)} %copy-done.205, ...), custom_call_target="tpu_custom_call" | custom-call | flops 16810770432 | bytes 34930688 | tf_op jit(solution)/shard_map/cond/branch_1_fun/head_stats/pallas_call | solution.py:220
  752.8 9.0 %all_gather.9 = f32[8,3,2,4,64]{4,3,2,1,0:T(4,128)S(1)} all-gather(f32[1,3,2,4,64]{4,3,2,1,0:T(4,128)S(1)} %copy.1005), channel_id=1, replica_groups=mesh['section'=4,'vocab'=2,'dp'=4] {'section','vocab'}, dimensions={0}, use_global_device_ids=true | all-gather | bytes 55296 | tf_op jit(solution)/shard_map/cond/branch_1_fun/all_gather | solution.py:464
  (532 shorter events, 305.2 us)
Async XLA Ops:
  51.7 41.0 %collective-permute-start.217 = (bf16[512,896]{0,1:T(8,128)(2,1)}, bf16[512,896]{0,1:T(8,128)(2,1)S(1)}, u32[]{:S(2)}, u32[]{:S(2)}) collective-permute-start(bf16[512,896]{0,1:T(8,128)(2,1)} %bitcast.436), channel_id=1, source_target_pairs={{0,16},{8,24},{16,0},{24,8},{1,17},{9,25},{17,1},{25,9},{2,18},{10... | collective-permute-start | bytes 2752520 | tf_op jit(solution)/shard_map/ppermute | solution.py:29
  53.0 39.6 %collective-permute-start.216 = (bf16[512,896]{0,1:T(8,128)(2,1)}, bf16[512,896]{0,1:T(8,128)(2,1)S(1)}, u32[]{:S(2)}, u32[]{:S(2)}) collective-permute-start(bf16[512,896]{0,1:T(8,128)(2,1)} %bitcast.435), channel_id=1, source_target_pairs={{0,24},{8,16},{16,8},{24,0},{1,25},{9,17},{17,9},{25,1},{2,26},{10... | collective-permute-start | bytes 2752520 | tf_op jit(solution)/shard_map/ppermute | solution.py:29
  55.3 40.1 %collective-permute-start.218 = (bf16[512,896]{0,1:T(8,128)(2,1)}, bf16[512,896]{0,1:T(8,128)(2,1)}, u32[]{:S(2)}, u32[]{:S(2)}) collective-permute-start(bf16[512,896]{0,1:T(8,128)(2,1)} %bitcast.437), channel_id=1, source_target_pairs={{0,8},{8,0},{16,24},{24,16},{1,9},{9,1},{17,25},{25,17},{2,10},{10... | collective-permute-start | bytes 2752520 | tf_op jit(solution)/shard_map/ppermute | solution.py:29
  66.1 39.4 %collective-permute-start.214 = (f32[1,2048]{1,0:T(1,128)S(1)}, f32[1,2048]{1,0:T(1,128)S(1)}, u32[]{:S(2)}, u32[]{:S(2)}) collective-permute-start(f32[1,2048]{1,0:T(1,128)S(1)} %copy-done.116), channel_id=1, source_target_pairs={{0,16},{8,24},{16,0},{24,8},{1,17},{9,25},{17,1},{25,9},{2,18},{10... | collective-permute-start | bytes 24584 | tf_op jit(solution)/shard_map/ppermute | solution.py:29
  95.3 51.0 %collective-permute-start.230 = (bf16[512,896]{0,1:T(8,128)(2,1)}, bf16[512,896]{0,1:T(8,128)(2,1)}, u32[]{:S(2)}, u32[]{:S(2)}) collective-permute-start(bf16[512,896]{0,1:T(8,128)(2,1)} %bitcast.438), channel_id=1, source_target_pairs={{0,16},{8,24},{16,0},{24,8},{1,17},{9,25},{17,1},{25,9},{2,18},{10... | collective-permute-start | bytes 2752520 | tf_op jit(solution)/shard_map/ppermute | solution.py:29
  102.9 47.3 %collective-permute-start.231 = (bf16[512,896]{0,1:T(8,128)(2,1)}, bf16[512,896]{0,1:T(8,128)(2,1)S(1)}, u32[]{:S(2)}, u32[]{:S(2)}) collective-permute-start(bf16[512,896]{0,1:T(8,128)(2,1)} %bitcast.127), channel_id=1, source_target_pairs={{0,24},{8,16},{16,8},{24,0},{1,25},{9,17},{17,9},{25,1},{2,26},{10... | collective-permute-start | bytes 2752520 | tf_op jit(solution)/shard_map/ppermute | solution.py:29
  106.5 43.7 %collective-permute-start.222 = (bf16[128,2048]{1,0:T(8,128)(2,1)}, bf16[128,2048]{1,0:T(8,128)(2,1)}, u32[]{:S(2)}, u32[]{:S(2)}) collective-permute-start(bf16[128,2048]{1,0:T(8,128)(2,1)} %fusion.122.refs_1_), channel_id=1, source_target_pairs={{0,4},{4,0},{1,5},{5,1},{2,6},{6,2},{3,7},{7,3},{8,12},{12,8},{9,1... | collective-permute-start | bytes 1572872 | tf_op jit(solution)/shard_map/ppermute | solution.py:29
  111.1 43.1 %collective-permute-start.221 = (bf16[128,2048]{1,0:T(8,128)(2,1)}, bf16[128,2048]{1,0:T(8,128)(2,1)S(1)}, u32[]{:S(2)}, u32[]{:S(2)}) collective-permute-start(bf16[128,2048]{1,0:T(8,128)(2,1)} %fusion.122.refs_1_), channel_id=1, source_target_pairs={{0,24},{8,16},{16,8},{24,0},{1,25},{9,17},{17,9},{25,1},{2,26},{10... | collective-permute-start | bytes 1572872 | tf_op jit(solution)/shard_map/ppermute | solution.py:29
  118.9 40.2 %collective-permute-start.220 = (bf16[128,2048]{1,0:T(8,128)(2,1)}, bf16[128,2048]{1,0:T(8,128)(2,1)S(1)}, u32[]{:S(2)}, u32[]{:S(2)}) collective-permute-start(bf16[128,2048]{1,0:T(8,128)(2,1)} %fusion.122.refs_1_), channel_id=1, source_target_pairs={{0,16},{8,24},{16,0},{24,8},{1,17},{9,25},{17,1},{25,9},{2,18},{10... | collective-permute-start | bytes 1572872 | tf_op jit(solution)/shard_map/ppermute | solution.py:29
  154.2 42.6 %collective-permute-start.237 = (bf16[896,512]{1,0:T(8,128)(2,1)S(1)}, bf16[896,512]{1,0:T(8,128)(2,1)S(1)}, u32[]{:S(2)}, u32[]{:S(2)}) collective-permute-start(bf16[896,512]{1,0:T(8,128)(2,1)S(1)} %get-tuple-element.1023), channel_id=1, source_target_pairs={{0,24},{8,16},{16,8},{24,0},{1,25},{9,17},{17,9},{25,1},{2,26},{10... | collective-permute-start | bytes 2752520 | tf_op jit(solution)/shard_map/ppermute | solution.py:29
  159.1 46.9 %collective-permute-start.226 = (bf16[1024,448]{0,1:T(8,128)(2,1)S(1)}, bf16[1024,448]{0,1:T(8,128)(2,1)S(1)}, u32[]{:S(2)}, u32[]{:S(2)}) collective-permute-start(bf16[1024,448]{0,1:T(8,128)(2,1)S(1)} %copy-done.42), channel_id=1, source_target_pairs={{0,1},{3,2},{4,5},{7,6},{8,9},{11,10},{12,13},{15,14},{16,17},{19,... | collective-permute-start | bytes 2752520 | tf_op jit(solution)/shard_map/ppermute | solution.py:29
  167.1 39.2 %collective-permute-start.227 = (bf16[1024,448]{0,1:T(8,128)(2,1)S(1)}, bf16[1024,448]{0,1:T(8,128)(2,1)S(1)}, u32[]{:S(2)}, u32[]{:S(2)}) collective-permute-start(bf16[1024,448]{0,1:T(8,128)(2,1)S(1)} %copy-done.41), channel_id=1, source_target_pairs={{0,2},{3,1},{4,6},{7,5},{8,10},{11,9},{12,14},{15,13},{16,18},{19,... | collective-permute-start | bytes 2752520 | tf_op jit(solution)/shard_map/ppermute | solution.py:29
  183.8 38.0 %collective-permute-start.225 = (bf16[128,2048]{1,0:T(8,128)(2,1)S(1)}, bf16[128,2048]{1,0:T(8,128)(2,1)S(1)}, u32[]{:S(2)}, u32[]{:S(2)}) collective-permute-start(bf16[128,2048]{1,0:T(8,128)(2,1)S(1)} %collective-permute-done.221.refs_4_), channel_id=1, source_target_pairs={{0,4},{4,0},{1,5},{5,1},{2,6},{6,2},{3,7},{7,3},{8,12},{12,8},{9,1... | collective-permute-start | bytes 1572872 | tf_op jit(solution)/shard_map/ppermute | solution.py:29
  206.7 37.7 %collective-permute-start.233 = (bf16[1024,448]{0,1:T(8,128)(2,1)S(1)}, bf16[1024,448]{0,1:T(8,128)(2,1)}, u32[]{:S(2)}, u32[]{:S(2)}) collective-permute-start(bf16[1024,448]{0,1:T(8,128)(2,1)S(1)} %pad_maximum_fusion.15), channel_id=1, source_target_pairs={{0,2},{3,1},{4,6},{7,5},{8,10},{11,9},{12,14},{15,13},{16,18},{19,... | collective-permute-start | bytes 2752520 | tf_op jit(solution)/shard_map/ppermute | solution.py:29
  340.9 65.6 %collective-permute-start.255 = (bf16[8,128]{1,0:T(8,128)(2,1)S(1)}, bf16[8,128]{1,0:T(8,128)(2,1)S(1)}, u32[]{:S(2)}, u32[]{:S(2)}) collective-permute-start(bf16[8,128]{1,0:T(8,128)(2,1)S(1)} %fusion.139), channel_id=1, source_target_pairs={{1,0},{2,3},{5,4},{6,7},{9,8},{10,11},{13,12},{14,15},{17,16},{18,... | collective-permute-start | bytes 6152 | tf_op jit(solution)/shard_map/ppermute | solution.py:414
  400.5 97.9 %collective-permute-start.252 = (bf16[512,896]{0,1:T(8,128)(2,1)}, bf16[512,896]{0,1:T(8,128)(2,1)}, u32[]{:S(2)}, u32[]{:S(2)}) collective-permute-start(bf16[512,896]{0,1:T(8,128)(2,1)} %get-tuple-element.1040), channel_id=1, source_target_pairs={{1,0},{2,3},{5,4},{6,7},{9,8},{10,11},{13,12},{14,15},{17,16},{18,... | collective-permute-start | bytes 2752520 | tf_op jit(solution)/shard_map/ppermute | solution.py:29
  401.8 99.9 %collective-permute-start.253 = (bf16[512,896]{0,1:T(8,128)(2,1)}, bf16[512,896]{0,1:T(8,128)(2,1)}, u32[]{:S(2)}, u32[]{:S(2)}) collective-permute-start(bf16[512,896]{0,1:T(8,128)(2,1)} %get-tuple-element.1041), channel_id=1, source_target_pairs={{1,3},{2,0},{5,7},{6,4},{9,11},{10,8},{13,15},{14,12},{17,19},{18,... | collective-permute-start | bytes 2752520 | tf_op jit(solution)/shard_map/ppermute | solution.py:29
  403.1 99.9 %collective-permute-start.254 = (bf16[512,896]{0,1:T(8,128)(2,1)}, bf16[512,896]{0,1:T(8,128)(2,1)}, u32[]{:S(2)}, u32[]{:S(2)}) collective-permute-start(bf16[512,896]{0,1:T(8,128)(2,1)} %get-tuple-element.1042), channel_id=1, source_target_pairs={{0,3},{3,0},{4,7},{7,4},{8,11},{11,8},{12,15},{15,12},{16,19},{19,... | collective-permute-start | bytes 2752520 | tf_op jit(solution)/shard_map/ppermute | solution.py:29
  406.5 150.9 %collective-permute-start.256 = (bf16[512,896]{0,1:T(8,128)(2,1)}, bf16[512,896]{0,1:T(8,128)(2,1)}, u32[]{:S(2)}, u32[]{:S(2)}) collective-permute-start(bf16[512,896]{0,1:T(8,128)(2,1)} %get-tuple-element.1043), channel_id=1, source_target_pairs={{1,0},{2,3},{5,4},{6,7},{9,8},{10,11},{13,12},{14,15},{17,16},{18,... | collective-permute-start | bytes 2752520 | tf_op jit(solution)/shard_map/ppermute | solution.py:29
  407.8 159.8 %collective-permute-start.257 = (bf16[512,896]{0,1:T(8,128)(2,1)}, bf16[512,896]{0,1:T(8,128)(2,1)}, u32[]{:S(2)}, u32[]{:S(2)}) collective-permute-start(bf16[512,896]{0,1:T(8,128)(2,1)} %get-tuple-element.1044), channel_id=1, source_target_pairs={{1,3},{2,0},{5,7},{6,4},{9,11},{10,8},{13,15},{14,12},{17,19},{18,... | collective-permute-start | bytes 2752520 | tf_op jit(solution)/shard_map/ppermute | solution.py:29
  498.4 69.2 %collective-permute-start.258 = (bf16[512,896]{0,1:T(8,128)(2,1)}, bf16[512,896]{0,1:T(8,128)(2,1)}, u32[]{:S(2)}, u32[]{:S(2)}) collective-permute-start(bf16[512,896]{0,1:T(8,128)(2,1)} %get-tuple-element.1045), channel_id=1, source_target_pairs={{0,3},{3,0},{4,7},{7,4},{8,11},{11,8},{12,15},{15,12},{16,19},{19,... | collective-permute-start | bytes 2752520 | tf_op jit(solution)/shard_map/ppermute | solution.py:29
  501.7 94.3 %collective-permute-start.259 = (bf16[896,512]{1,0:T(8,128)(2,1)}, bf16[896,512]{1,0:T(8,128)(2,1)}, u32[]{:S(2)}, u32[]{:S(2)}) collective-permute-start(bf16[896,512]{1,0:T(8,128)(2,1)} %get-tuple-element.1046), channel_id=1, source_target_pairs={{1,0},{2,3},{5,4},{6,7},{9,8},{10,11},{13,12},{14,15},{17,16},{18,... | collective-permute-start | bytes 2752520 | tf_op jit(solution)/shard_map/ppermute | solution.py:29
  503.1 93.0 %collective-permute-start.260 = (bf16[896,512]{1,0:T(8,128)(2,1)}, bf16[896,512]{1,0:T(8,128)(2,1)}, u32[]{:S(2)}, u32[]{:S(2)}) collective-permute-start(bf16[896,512]{1,0:T(8,128)(2,1)} %get-tuple-element.1047), channel_id=1, source_target_pairs={{1,3},{2,0},{5,7},{6,4},{9,11},{10,8},{13,15},{14,12},{17,19},{18,... | collective-permute-start | bytes 2752520 | tf_op jit(solution)/shard_map/ppermute | solution.py:29
  557.4 38.7 %collective-permute-start.261 = (bf16[896,512]{1,0:T(8,128)(2,1)}, bf16[896,512]{1,0:T(8,128)(2,1)}, u32[]{:S(2)}, u32[]{:S(2)}) collective-permute-start(bf16[896,512]{1,0:T(8,128)(2,1)} %get-tuple-element.1048), channel_id=1, source_target_pairs={{0,3},{3,0},{4,7},{7,4},{8,11},{11,8},{12,15},{15,12},{16,19},{19,... | collective-permute-start | bytes 2752520 | tf_op jit(solution)/shard_map/ppermute | solution.py:29
  (167 other events, 2817.4 us)
